TPU v7x, 32 devices: a whole 2x2x4 slice. The times are simulated.
32 devices in a mesh: row: 4 (over y, x), col: 8 (over z, core).
Axes of the slice: x: 2, y: 2, z: 4, core: 2. Of those that a mesh axis runs over, the one named last changes fastest.
Arguments:
- adjacency: int32 [8192, 256], P('row', 'col'), may hold values from -2147483648 to 2147483647, as said below
- seed_mask: int32 [8192], P('col'), may hold values 0 or 1
- source: int32 [1], replicated, may hold values from 0 to 8191
Outputs:
- levels: int32 [8192], P('col')
- parents: int32 [8192], P('col')
Inputs may be any that keep to these rules, and one draw needn't show every extreme that they name: adjacency is symmetric (edge(u, v) = edge(v, u)); it is the union of 131072 Kronecker edges whose endpoints pick one of four quadrants per bit with weights 57, 19, 19, 5 out of 100, vertex labels not permuted, so low ids carry most edges; each word is a 32-bit pattern read as a signed int32.
All inputs are finite; a program needn't handle non-finite values.
Results may differ from a plain program's by a relative error of at most 0.000001.
Values may be sent and summed in bfloat16 or wider, within the bound.
A program may use at most 64 MiB of HBM per device.

v0:
```python
import math
import jax
import jax.numpy as jnp
from jax import lax
from jax.sharding import PartitionSpec as P

LEVELS = 4
absent = 1073741824


def from_root(block, axis, source):
    block = jnp.where(lax.axis_index(axis) == source, block, jnp.zeros_like(block))
    return lax.psum(block, axis)


def unpack(words):
    shifts = jnp.arange(32, dtype=jnp.int32)
    bit_table = jnp.bitwise_and(jnp.right_shift(words[..., None], shifts), 1)
    return bit_table.reshape(words.shape[:-1] + (words.shape[-1] * 32,))


def nearest_sources(adjacency, active, first_row):
    height = adjacency.shape[0]
    width = adjacency.shape[1] * 32
    block_rows = math.gcd(height, 256)

    def sweep_block(lowest, block_id):
        offset = block_id * block_rows
        tile_words = lax.dynamic_slice_in_dim(adjacency, offset, block_rows, 0)
        marks = lax.dynamic_slice_in_dim(active, offset, block_rows, 0)

        def scan_tile(current):
            row_ids = first_row + offset + jnp.arange(block_rows, dtype=jnp.int32)
            linked = unpack(tile_words) * marks[:, None] > 0
            found = jnp.min(jnp.where(linked, row_ids[:, None], absent), axis=0)
            return jnp.minimum(current, found)

        def keep_tile(current):
            return current

        lowest = lax.cond(jnp.any(marks > 0), scan_tile, keep_tile, lowest)
        return (lowest, None)

    start_value = jnp.full((width,), absent, jnp.int32)
    lowest, unused = lax.scan(
        sweep_block, start_value, jnp.arange(height // block_rows, dtype=jnp.int32)
    )
    return lowest


def row_frontier_of(frontier):
    col_count = lax.axis_size("col")
    row_count = lax.axis_size("row")
    owner_count = col_count // row_count
    blocks = []
    for part_no in range(owner_count):
        root_col = lax.axis_index("row") * owner_count + part_no
        blocks.append(from_root(frontier, "col", root_col))
    row_payload = jnp.concatenate(blocks, axis=0)
    return row_payload


def local(adjacency, seed_mask, source):
    height = adjacency.shape[0]
    width = adjacency.shape[1] * 32
    first_row = (lax.axis_index("row") * height).astype(jnp.int32)
    first_col = (lax.axis_index("col") * width).astype(jnp.int32)
    vertex_ids = first_col + jnp.arange(width, dtype=jnp.int32)
    reached = (seed_mask > 0) | (vertex_ids == source[0])
    levels = jnp.where(reached, 0, -1).astype(jnp.int32)
    parents = jnp.where(reached, vertex_ids, -1).astype(jnp.int32)
    frontier = reached.astype(jnp.int32)
    for depth_no in range(1, LEVELS + 1):
        row_frontier = row_frontier_of(frontier)
        nearest = nearest_sources(adjacency, row_frontier, first_row)
        nearest = lax.pmin(nearest, "row")
        fresh = (nearest < absent) & (levels < 0)
        levels = jnp.where(fresh, depth_no, levels).astype(jnp.int32)
        parents = jnp.where(fresh, nearest, parents).astype(jnp.int32)
        frontier = fresh.astype(jnp.int32)
    return (levels, parents)


def solution(mesh):
    in_specs = (P("row", "col"), P("col"), P())
    out_specs = (P("col"), P("col"))
    return jax.shard_map(local, mesh=mesh, in_specs=in_specs, out_specs=out_specs, check_vma=False)
```

profile of v0, /device:TPU:0, one launch (start us, length us, event | category | flops | bytes accessed | tf_op | source)
XLA Modules:
  0.0 188.8 jit_solution(4440167789065246323)
XLA Ops:
  1.4 10.8 %all-reduce.3 = (s32[1024]{0:T(1024)S(1)}, s32[1024]{0:T(1024)S(1)}) all-reduce(s32[1024]{0:T(1024)S(1)} %convert_select_fusion.6, s32[1024]{0:T(1024)S(1)} %get-tuple-element.372), channel_id=1, replica_groups=mesh['row'=4,'col'=8] {'col'}, use_global_device_ids=true, to_apply=%region_1.2 | all-reduce | flops 2048 | bytes 16384 | tf_op jit(solution)/shard_map/psum | solution.py:13
  12.2 24.8 %while.52 = (s32[]{:T(128)}, s32[1024]{0:T(1024)S(1)}, s32[8]{0:T(128)S(1)}, s32[2048]{0:T(1024)S(1)}, s32[2048,32]{0,1:T(8,128)}, /*index=5*/s32[]{:T(128)}, s32[]{:T(128)}, s32[1]{0:T(128)}, s32[]{:T(128)}, s32[]{:T(128)}) while((s32[]{:T(128)}, s32[1024]{0:T(1024)S(1)}, s32[8]{0:T(128)S(1)}, s32[2048]{0:T(1024)S(1)}, s32[2048,32]{0,1:T(8,128)}, ...), condition=%wide.region_7.8_spmd, body=%wide.region_2.7_spmd.sunk | while | flops 1573639 | bytes 128245 | solution.py:45
  20.3 1.6 conditional.8
  29.9 1.6 conditional.8
  37.0 8.9 %pmin.28 = s32[1024]{0:T(1024)S(1)} all-reduce(s32[1024]{0:T(1024)S(1)} %get-tuple-element.274), channel_id=1, replica_groups=mesh['row'=4,'col'=8] {'row'}, use_global_device_ids=true, to_apply=%region_8.9 | all-reduce | flops 1024 | bytes 8192 | tf_op jit(solution)/shard_map/pmin | solution.py:76
  45.9 6.3 %all-reduce.2 = (s32[1024]{0:T(1024)S(1)}, s32[1024]{0:T(1024)S(1)}) all-reduce(s32[1024]{0:T(1024)S(1)} %convert_select_fusion.4, s32[1024]{0:T(1024)S(1)} %get-tuple-element.370), channel_id=1, replica_groups=mesh['row'=4,'col'=8] {'col'}, use_global_device_ids=true, to_apply=%region_10.11 | all-reduce | flops 2048 | bytes 16384 | tf_op jit(solution)/shard_map/psum | solution.py:13
  52.3 32.7 %while.53 = (s32[]{:T(128)}, s32[1024]{0:T(1024)S(1)}, s32[8]{0:T(128)S(1)}, s32[2048]{0:T(1024)S(1)}, s32[2048,32]{0,1:T(8,128)}, /*index=5*/s32[]{:T(128)}, s32[]{:T(128)}, s32[1]{0:T(128)}, s32[]{:T(128)}, s32[]{:T(128)}) while((s32[]{:T(128)}, s32[1024]{0:T(1024)S(1)}, s32[8]{0:T(128)S(1)}, s32[2048]{0:T(1024)S(1)}, ...), condition=%wide.region_16.17_spmd, body=%wide.region_11.16_spmd.sunk | while | flops 1573639 | bytes 128245 | solution.py:45
  55.0 1.6 conditional.9
  59.3 1.6 conditional.9
  63.5 1.6 conditional.9
  67.8 1.6 conditional.9
  72.1 1.6 conditional.9
  76.4 1.6 conditional.9
  80.7 1.6 conditional.9
  85.0 5.6 %pmin.29 = s32[1024]{0:T(1024)S(1)} all-reduce(s32[1024]{0:T(1024)S(1)} %get-tuple-element.275), channel_id=1, replica_groups=mesh['row'=4,'col'=8] {'row'}, use_global_device_ids=true, to_apply=%region_17.18 | all-reduce | flops 1024 | bytes 8192 | tf_op jit(solution)/shard_map/pmin | solution.py:76
  90.6 8.9 %all-reduce.1 = (s32[1024]{0:T(1024)S(1)}, s32[1024]{0:T(1024)S(1)}) all-reduce(s32[1024]{0:T(1024)S(1)} %convert_select_fusion.2, s32[1024]{0:T(1024)S(1)} %get-tuple-element.368), channel_id=1, replica_groups=mesh['row'=4,'col'=8] {'col'}, use_global_device_ids=true, to_apply=%region_19.20 | all-reduce | flops 2048 | bytes 16384 | tf_op jit(solution)/shard_map/psum | solution.py:13
  99.5 34.2 %while.54 = (s32[]{:T(128)}, s32[1024]{0:T(1024)S(1)}, s32[8]{0:T(128)S(1)}, s32[2048]{0:T(1024)S(1)}, s32[2048,32]{0,1:T(8,128)}, /*index=5*/s32[]{:T(128)}, s32[]{:T(128)}, s32[1]{0:T(128)}, s32[]{:T(128)}, s32[]{:T(128)}) while((s32[]{:T(128)}, s32[1024]{0:T(1024)S(1)}, s32[8]{0:T(128)S(1)}, s32[2048]{0:T(1024)S(1)}, ...), condition=%wide.region_25.26_spmd, body=%wide.region_20.25_spmd.sunk | while | flops 1573639 | bytes 128245 | solution.py:45
  102.2 1.6 conditional.10
  106.5 1.6 conditional.10
  110.8 1.6 conditional.10
  115.1 1.6 conditional.10
  119.3 1.6 conditional.10
  123.6 1.6 conditional.10
  127.9 1.6 conditional.10
  133.8 8.2 %pmin.30 = s32[1024]{0:T(1024)S(1)} all-reduce(s32[1024]{0:T(1024)S(1)} %get-tuple-element.276), channel_id=1, replica_groups=mesh['row'=4,'col'=8] {'row'}, use_global_device_ids=true, to_apply=%region_26.27 | all-reduce | flops 1024 | bytes 8192 | tf_op jit(solution)/shard_map/pmin | solution.py:76
  141.9 6.4 %all-reduce = (s32[1024]{0:T(1024)S(1)}, s32[1024]{0:T(1024)S(1)}) all-reduce(s32[1024]{0:T(1024)S(1)} %convert_select_fusion, s32[1024]{0:T(1024)S(1)} %get-tuple-element.366), channel_id=1, replica_groups=mesh['row'=4,'col'=8] {'col'}, use_global_device_ids=true, to_apply=%region_28.29 | all-reduce | flops 2048 | bytes 16384 | tf_op jit(solution)/shard_map/psum | solution.py:13
  148.4 34.2 %while.55 = (s32[]{:T(128)}, s32[1024]{0:T(1024)S(1)}, s32[8]{0:T(128)S(1)}, s32[2048]{0:T(1024)S(1)}, s32[2048,32]{0,1:T(8,128)}, /*index=5*/s32[]{:T(128)}, s32[]{:T(128)}, s32[1]{0:T(128)}, s32[]{:T(128)}, s32[]{:T(128)}) while((s32[]{:T(128)}, s32[1024]{0:T(1024)S(1)}, s32[8]{0:T(128)S(1)}, s32[2048]{0:T(1024)S(1)}, ...), condition=%wide.region_34.35_spmd, body=%wide.region_29.34_spmd.sunk | while | flops 1573639 | bytes 128245 | solution.py:45
  151.0 1.6 conditional.11
  155.3 1.6 conditional.11
  159.6 1.6 conditional.11
  163.9 1.6 conditional.11
  182.6 5.6 %pmin.31 = s32[1024]{0:T(1024)S(1)} all-reduce(s32[1024]{0:T(1024)S(1)} %get-tuple-element.277), channel_id=1, replica_groups=mesh['row'=4,'col'=8] {'row'}, use_global_device_ids=true, to_apply=%region_35.36 | all-reduce | flops 1024 | bytes 8192 | tf_op jit(solution)/shard_map/pmin | solution.py:76
  (224 shorter events, 92.7 us)
Async XLA Ops:
  0.6 0.7 copy-start
where the time goes:
time: 191 us; the launch traced here: 189 us
  blocking collectives  60.7 us (32%)
  local copies, waits for them, and re-layouts  44.5 us (23%)
  loops' own time  42 us (22%)
  other arithmetic  40.1 us (21%)
    another operation x4, loops' own time, nearest_sources(): lax.scan(sweep_block, start_value, jnp.arange(height // block_rows, dtype...  41.3 us
    psum x4, blocking collectives, from_root(): return lax.psum(block, axis)  32.4 us
    pmin x4, blocking collectives, local(): nearest = lax.pmin(nearest, 'row')  28.3 us
    reduce_or x32, other arithmetic, sweep_block(): lowest = lax.cond(jnp.any(marks > 0), scan_tile, keep_tile, lowest)  23.5 us
    dynamic_slice x25, local copies, waits for them, and re-layouts, sweep_block(): tile_words = lax.dynamic_slice_in_dim(adjacency, offset, block_rows, 0)  22 us
    dynamic_slice x32, local copies, waits for them, and re-layouts, nearest_sources(): lax.scan(sweep_block, start_value, jnp.arange(height // block_rows, dtype...  20.7 us
    reduce_min x25, other arithmetic, scan_tile(): found = jnp.min(jnp.where(linked, row_ids[:, None], absent), axis=0)  15.6 us

commit v1 on v0

--- a/solution.py
+++ b/solution.py
@@ -8,9 +8,15 @@
 absent = 1073741824
 
 
+def add_all(x, axis):
+    pieces = lax.all_gather(x, axis, axis=0, tiled=False)
+    result = pieces.sum(axis=0)
+    return result
+
+
 def from_root(block, axis, source):
     block = jnp.where(lax.axis_index(axis) == source, block, jnp.zeros_like(block))
-    return lax.psum(block, axis)
+    return add_all(block, axis)
 
 
 def unpack(words):

time: 191 us -> 252 us (1.32)
  blocking collectives: 60.7 us -> 142 us
  local copies, waits for them, and re-layouts: 44.5 us -> 24.8 us
    all_gather x0 -> x8, blocking collectives: none -> 114 us  [add_all(): pieces = lax.all_gather(x, axis, axis=0, tiled=False)]
    psum x4 -> x0, blocking collectives: 32.4 us -> none  [from_root(): return lax.psum(block, axis)]
    dynamic_slice x25, local copies, waits for them, and re-layouts: 22 us -> 2.09 us  [sweep_block(): tile_words = lax.dynamic_slice_in_dim(adjacency, offset, block_rows, 0)]
where the time goes in v1:
time: 252 us; the launch traced here: 251 us
  blocking collectives  142 us (56%)
  loops' own time  42 us (17%)
  other arithmetic  40.8 us (16%)
  local copies, waits for them, and re-layouts  24.8 us (10%)
    all_gather x8, blocking collectives, add_all(): pieces = lax.all_gather(x, axis, axis=0, tiled=False)  114 us
    another operation x4, loops' own time, nearest_sources(): lax.scan(sweep_block, start_value, jnp.arange(height // block_rows, dtype...  41.3 us
    pmin x4, blocking collectives, local(): nearest = lax.pmin(nearest, 'row')  27.6 us
    reduce_or x32, other arithmetic, sweep_block(): lowest = lax.cond(jnp.any(marks > 0), scan_tile, keep_tile, lowest)  23.5 us
    dynamic_slice x32, local copies, waits for them, and re-layouts, nearest_sources(): lax.scan(sweep_block, start_value, jnp.arange(height // block_rows, dtype...  20.7 us
    reduce_min x25, other arithmetic, scan_tile(): found = jnp.min(jnp.where(linked, row_ids[:, None], absent), axis=0)  15.6 us

profile of v1, /device:TPU:0, one launch (start us, length us, event | category | flops | bytes accessed | tf_op | source)
XLA Modules:
  0.0 251.1 jit_solution(10301967488449996640)
XLA Ops:
  2.0 15.8 %all-gather.1 = s32[8192]{0:T(1024)S(1)} all-gather(s32[1024]{0:T(1024)S(1)} %convert_select_fusion.6), channel_id=3, replica_groups=mesh['row'=4,'col'=8] {'col'}, dimensions={0}, use_global_device_ids=true | all-gather | bytes 36864 | tf_op jit(solution)/shard_map/all_gather | solution.py:12
  17.9 14.1 %all-gather = s32[8192]{0:T(1024)S(1)} all-gather(s32[1024]{0:T(1024)S(1)} %get-tuple-element.388), channel_id=2, replica_groups=mesh['row'=4,'col'=8] {'col'}, dimensions={0}, use_global_device_ids=true | all-gather | bytes 36864 | tf_op jit(solution)/shard_map/all_gather | solution.py:12
  32.0 23.2 %while.52 = (s32[]{:T(128)}, s32[1024]{0:T(1024)S(1)}, s32[8]{0:T(128)S(1)}, s32[2048]{0:T(1024)S(1)}, s32[2048,32]{0,1:T(8,128)S(1)}, /*index=5*/s32[]{:T(128)}, s32[]{:T(128)}, s32[1]{0:T(128)}, s32[]{:T(128)}, s32[]{:T(128)}) while((s32[]{:T(128)}, s32[1024]{0:T(1024)S(1)}, s32[8]{0:T(128)S(1)}, s32[2048]{0:T(1024)S(1)}, ...), condition=%wide.region_7.8_spmd, body=%wide.region_2.7_spmd.sunk | while | flops 1573639 | bytes 128245 | solution.py:51
  40.1 0.8 conditional.8
  55.2 8.2 %pmin.28 = s32[1024]{0:T(1024)S(1)} all-reduce(s32[1024]{0:T(1024)S(1)} %get-tuple-element.274), channel_id=1, replica_groups=mesh['row'=4,'col'=8] {'row'}, use_global_device_ids=true, to_apply=%region_8.9 | all-reduce | flops 1024 | bytes 8192 | tf_op jit(solution)/shard_map/pmin | solution.py:82
  63.4 14.1 %all-gather.3 = s32[8192]{0:T(1024)S(1)} all-gather(s32[1024]{0:T(1024)S(1)} %convert_select_fusion.4), channel_id=5, replica_groups=mesh['row'=4,'col'=8] {'col'}, dimensions={0}, use_global_device_ids=true | all-gather | bytes 36864 | tf_op jit(solution)/shard_map/all_gather | solution.py:12
  77.6 14.1 %all-gather.2 = s32[8192]{0:T(1024)S(1)} all-gather(s32[1024]{0:T(1024)S(1)} %get-tuple-element.386), channel_id=4, replica_groups=mesh['row'=4,'col'=8] {'col'}, dimensions={0}, use_global_device_ids=true | all-gather | bytes 36864 | tf_op jit(solution)/shard_map/all_gather | solution.py:12
  91.7 27.1 %while.53 = (s32[]{:T(128)}, s32[1024]{0:T(1024)S(1)}, s32[8]{0:T(128)S(1)}, s32[2048]{0:T(1024)S(1)}, s32[2048,32]{0,1:T(8,128)S(1)}, /*index=5*/s32[]{:T(128)}, s32[]{:T(128)}, s32[1]{0:T(128)}, s32[]{:T(128)}, s32[]{:T(128)}) while((s32[]{:T(128)}, s32[1024]{0:T(1024)S(1)}, s32[8]{0:T(128)S(1)}, s32[2048]{0:T(1024)S(1)}, ...), condition=%wide.region_16.17_spmd, body=%wide.region_11.16_spmd.sunk | while | flops 1573639 | bytes 128245 | solution.py:51
  94.4 0.8 conditional.9
  97.9 0.8 conditional.9
  101.4 0.8 conditional.9
  104.8 0.8 conditional.9
  108.3 0.8 conditional.9
  111.8 0.8 conditional.9
  115.3 0.8 conditional.9
  118.8 5.6 %pmin.29 = s32[1024]{0:T(1024)S(1)} all-reduce(s32[1024]{0:T(1024)S(1)} %get-tuple-element.275), channel_id=1, replica_groups=mesh['row'=4,'col'=8] {'row'}, use_global_device_ids=true, to_apply=%region_17.18 | all-reduce | flops 1024 | bytes 8192 | tf_op jit(solution)/shard_map/pmin | solution.py:82
  124.4 14.1 %all-gather.5 = s32[8192]{0:T(1024)S(1)} all-gather(s32[1024]{0:T(1024)S(1)} %convert_select_fusion.2), channel_id=7, replica_groups=mesh['row'=4,'col'=8] {'col'}, dimensions={0}, use_global_device_ids=true | all-gather | bytes 36864 | tf_op jit(solution)/shard_map/all_gather | solution.py:12
  138.6 14.1 %all-gather.4 = s32[8192]{0:T(1024)S(1)} all-gather(s32[1024]{0:T(1024)S(1)} %get-tuple-element.384), channel_id=6, replica_groups=mesh['row'=4,'col'=8] {'col'}, dimensions={0}, use_global_device_ids=true | all-gather | bytes 36864 | tf_op jit(solution)/shard_map/all_gather | solution.py:12
  152.7 27.9 %while.54 = (s32[]{:T(128)}, s32[1024]{0:T(1024)S(1)}, s32[8]{0:T(128)S(1)}, s32[2048]{0:T(1024)S(1)}, s32[2048,32]{0,1:T(8,128)S(1)}, /*index=5*/s32[]{:T(128)}, s32[]{:T(128)}, s32[1]{0:T(128)}, s32[]{:T(128)}, s32[]{:T(128)}) while((s32[]{:T(128)}, s32[1024]{0:T(1024)S(1)}, s32[8]{0:T(128)S(1)}, s32[2048]{0:T(1024)S(1)}, ...), condition=%wide.region_25.26_spmd, body=%wide.region_20.25_spmd.sunk | while | flops 1573639 | bytes 128245 | solution.py:51
  155.4 0.8 conditional.10
  158.9 0.8 conditional.10
  162.4 0.8 conditional.10
  165.9 0.8 conditional.10
  169.3 0.8 conditional.10
  172.8 0.8 conditional.10
  176.3 0.8 conditional.10
  179.8 0.8 conditional.10
  180.6 8.2 %pmin.30 = s32[1024]{0:T(1024)S(1)} all-reduce(s32[1024]{0:T(1024)S(1)} %get-tuple-element.276), channel_id=1, replica_groups=mesh['row'=4,'col'=8] {'row'}, use_global_device_ids=true, to_apply=%region_26.27 | all-reduce | flops 1024 | bytes 8192 | tf_op jit(solution)/shard_map/pmin | solution.py:82
  188.8 14.1 %all-gather.7 = s32[8192]{0:T(1024)S(1)} all-gather(s32[1024]{0:T(1024)S(1)} %convert_select_fusion), channel_id=9, replica_groups=mesh['row'=4,'col'=8] {'col'}, dimensions={0}, use_global_device_ids=true | all-gather | bytes 36864 | tf_op jit(solution)/shard_map/all_gather | solution.py:12
  202.9 14.1 %all-gather.6 = s32[8192]{0:T(1024)S(1)} all-gather(s32[1024]{0:T(1024)S(1)} %get-tuple-element.382), channel_id=8, replica_groups=mesh['row'=4,'col'=8] {'col'}, dimensions={0}, use_global_device_ids=true | all-gather | bytes 36864 | tf_op jit(solution)/shard_map/all_gather | solution.py:12
  217.1 27.9 %while.55 = (s32[]{:T(128)}, s32[1024]{0:T(1024)S(1)}, s32[8]{0:T(128)S(1)}, s32[2048]{0:T(1024)S(1)}, s32[2048,32]{0,1:T(8,128)S(1)}, /*index=5*/s32[]{:T(128)}, s32[]{:T(128)}, s32[1]{0:T(128)}, s32[]{:T(128)}, s32[]{:T(128)}) while((s32[]{:T(128)}, s32[1024]{0:T(1024)S(1)}, s32[8]{0:T(128)S(1)}, s32[2048]{0:T(1024)S(1)}, ...), condition=%wide.region_34.35_spmd, body=%wide.region_29.34_spmd.sunk | while | flops 1573639 | bytes 128245 | solution.py:51
  244.9 5.6 %pmin.31 = s32[1024]{0:T(1024)S(1)} all-reduce(s32[1024]{0:T(1024)S(1)} %get-tuple-element.277), channel_id=1, replica_groups=mesh['row'=4,'col'=8] {'row'}, use_global_device_ids=true, to_apply=%region_35.36 | all-reduce | flops 1024 | bytes 8192 | tf_op jit(solution)/shard_map/pmin | solution.py:82
  (244 shorter events, 73.0 us)
Async XLA Ops:
  0.6 31.4 %copy-start = (s32[2048,32]{0,1:T(8,128)S(1)}, s32[2048,32]{0,1:T(8,128)}, u32[]{:S(2)}) copy-start(s32[2048,32]{0,1:T(8,128)} %param.19) | copy-start | bytes 786436
